TPU v7x, 32 devices: a whole 2x2x4 slice. The times are simulated.
32 devices in a mesh: gene: 8 (over z, x), cell: 4 (over y, core).
Axes of the slice: x: 2, y: 2, z: 4, core: 2. Of those that a mesh axis runs over, the one named last changes fastest.
Arguments:
- counts: bfloat16 [32768, 8192], P('gene', 'cell'), may hold values from -6 to 6
- loadings: float32 [32768, 128], P('gene'), may hold values from -0.03125 to 0.03125
- values: float32 [128], replicated, may hold values from 0.5 to 2
- test_matrix: bfloat16 [8192, 128], P('cell'), may hold values from -0.0625 to 0.0625
- tile_mask: int32 [128, 64], P('gene', 'cell'), may hold values 0 or 1
Outputs:
- new_loadings: float32 [32768, 128], P('gene')
- new_values: float32 [128], replicated
All inputs are finite; a program needn't handle non-finite values. No bound on the sum of `tile_mask` on one device may be relied on, other than what follows from the above.
Results may differ from a plain program's by a relative error of at most 0.0028.
Values sent between devices are 32-bit elements; how exact they have to be, the bound alone decides.
A program may use at most 128 MiB of HBM per device.

v0:
```python
import jax
import jax.numpy as jnp
from jax import lax
from jax.sharding import PartitionSpec as P

GENE_TILE = 256
CELL_TILE = 128
SWEEPS = 3


def contract(left, right):
    return lax.dot_general(
        left,
        right,
        (((0,), (0,)), ((), ())),
        precision=lax.Precision.HIGHEST,
        preferred_element_type=jnp.float32,
    )


def outer_rows(stacked):
    return lax.dot_general(
        stacked,
        stacked,
        (((1,), (1,)), ((), ())),
        precision=lax.Precision.HIGHEST,
        preferred_element_type=jnp.float32,
    )


def local(counts, loadings, values, test_matrix, tile_mask):
    highest = lax.Precision.HIGHEST
    gene_rows, cell_cols = counts.shape
    components = loadings.shape[1]
    sketch_width = test_matrix.shape[1]
    cells_total = cell_cols * lax.axis_size("cell")
    genes_total = gene_rows * lax.axis_size("gene")
    tile_wide = jnp.repeat(
        jnp.repeat(tile_mask.astype(jnp.bfloat16), GENE_TILE, axis=0), CELL_TILE, axis=1
    )
    masked = counts * tile_wide
    load_narrow = loadings.astype(jnp.bfloat16)
    proj_part = lax.dot_general(
        load_narrow, masked, (((0,), (0,)), ((), ())), preferred_element_type=jnp.float32
    )
    projection = lax.psum(proj_part, "gene")
    test_wide = test_matrix.astype(jnp.float32)
    raw_part = jnp.dot(masked, test_matrix, preferred_element_type=jnp.float32)
    small_part = jnp.dot(projection, test_wide, precision=highest)
    raw_sketch, small_sketch = lax.psum((raw_part, small_part), "cell")
    sketch = raw_sketch - jnp.dot(loadings, small_sketch, precision=highest)
    sketch_gram = lax.psum(contract(sketch, sketch), "gene")
    factor = jnp.linalg.cholesky(sketch_gram)
    basis_rows = jax.scipy.linalg.solve_triangular(factor, sketch.T, lower=True)
    along_loadings = jnp.dot(basis_rows, loadings, precision=highest)
    coef = lax.psum(
        jnp.dot(basis_rows, masked, precision=highest, preferred_element_type=jnp.float32)
        - jnp.dot(along_loadings, projection, precision=highest),
        "gene",
    )
    stacked = jnp.concatenate([projection, coef], axis=0)
    core_sum = lax.psum(outer_rows(stacked), "cell")
    squares = jnp.concatenate([values * values, jnp.zeros((sketch_width,), jnp.float32)])
    core_matrix = core_sum / cells_total + jnp.diag(squares)
    subspace = jnp.eye(components + sketch_width, components, dtype=jnp.float32)
    for sweep in range(SWEEPS):
        image_block = jnp.dot(core_matrix, subspace, precision=highest)
        chol = jnp.linalg.cholesky(contract(image_block, image_block))
        subspace = jax.scipy.linalg.solve_triangular(chol, image_block.T, lower=True).T
    final_image = jnp.dot(core_matrix, subspace, precision=highest)
    new_values = jnp.sqrt(jnp.sum(subspace * final_image, axis=0))
    rotated = jnp.dot(loadings, subspace[:components], precision=highest) + contract(
        basis_rows, subspace[components:]
    )
    new_loadings = rotated * genes_total**0.5
    return (new_loadings, new_values)


def solution(mesh):
    placed = (P("gene", "cell"), P("gene", None), P(), P("cell", None), P("gene", "cell"))
    return jax.shard_map(
        local, mesh=mesh, in_specs=placed, out_specs=(P("gene", None), P()), check_vma=False
    )
```

profile of v0, /device:TPU:0, one launch (start us, length us, event | category | flops | bytes accessed | tf_op | source)
XLA Modules:
  0.0 522.0 jit_solution(2787085083832913234)
XLA Ops:
  7.2 0.7 convert_element_type.8
  8.1 19.0 %broadcast_in_dim.27 = bf16[4096,16,128]{2,1,0:T(8,128)(2,1)} broadcast(bf16[4096,16]{1,0:T(8,128)(2,1)S(1)} %bitcast.89), dimensions={0,1} | broadcast | bytes 16908288 | tf_op jit(solution)/shard_map/broadcast_in_dim | solution.py:38
  27.1 14.2 %convolution_bitcast_fusion.2 = f32[128,2048]{0,1:T(8,128)} fusion(f32[4096,128]{1,0:T(8,128)S(1)} %copy-done.1, bf16[4096,2048]{1,0:T(8,128)(2,1)} %param.8, bf16[512,8,16,128]{3,2,1,0:T(8,128)(2,1)} %bitcast.86), kind=kOutput, calls=%fused_computation.7 | convolution fusion | flops 2156396544 | bytes 36700160 | tf_op jit(solution)/shard_map/dot_general | solution.py:43
  41.3 15.6 %fusion.40 = f32[4096,128]{1,0:T(8,128)} fusion(bf16[2048,128]{1,0:T(8,128)(2,1)S(1)} %copy-done, bf16[4096,2048]{1,0:T(8,128)(2,1)} %param.8, bf16[512,8,16,128]{3,2,1,0:T(8,128)(2,1)} %bitcast.87), kind=kOutput, calls=%fused_computation.65 | convolution fusion | flops 2155872256 | bytes 36175872 | tf_op jit(solution)/shard_map/dot_general | solution.py:48
  56.9 65.6 %all-reduce.8.cloned.1.call-done = f32[128,2048]{0,1:T(8,128)} async-done(((f32[128,2048]{0,1:T(8,128)}), f32[128,2048]{0,1:T(8,128)}) %all-reduce.8.cloned.1.call-update) | async-done | bytes 1048592 | tf_op jit(solution)/shard_map/psum | solution.py:46
  122.5 2.8 fusion.41
  125.4 0.6 all-reduce.10.cloned.1.call-start
  126.0 51.7 %all-reduce.16.cloned.1.call-done = (f32[4096,128]{1,0:T(8,128)}, f32[128,128]{1,0:T(8,128)}) async-done(((f32[4096,128]{1,0:T(8,128)}, f32[128,128]{1,0:T(8,128)}), (f32[4096,128]{1,0:T(8,128)}, f32[128,128]{1,0:T(8,128)})) %all-reduce.16.cloned.1.call-update) | async-done | bytes 2162704 | tf_op jit(solution)/shard_map/psum | solution.py:50
  177.7 4.0 fusion.1
  181.7 4.1 fusion.42
  186.0 69.3 %all-reduce.10.cloned.1.call-done = f32[128,128]{0,1:T(8,128)} async-done(((f32[128,128]{0,1:T(8,128)}), f32[128,128]{0,1:T(8,128)}) %all-reduce.10.cloned.1.call-update) | async-done | bytes 65552 | tf_op jit(solution)/shard_map/psum | solution.py:52
  255.3 0.9 copy.9
  256.3 0.9 fusion.29
  257.1 11.7 %cholesky.74 = f32[128,128]{1,0:T(8,128)S(1)} custom-call(f32[128,128]{1,0:T(8,128)S(1)} %fusion.29), custom_call_target="Cholesky" | custom-call | tf_op jit(solution)/shard_map/jit(cholesky)/cholesky | solution.py:53
  268.9 0.6 compare_reduce_fusion.3
  269.5 0.7 fusion.15
  270.2 9.8 %custom-call.9 = f32[1,128,128]{1,2,0:T(8,128)S(1)} custom-call(f32[1,128,128]{2,1,0:T(8,128)S(1)} %fusion.15), custom_call_target="InvertDiagBlocksLowerTriangular" | custom-call | tf_op jit(solution)/shard_map/jit(_solve_triangular)/triangular_solve | solution.py:54
  280.0 3.3 fusion.27
  283.2 27.7 %fusion.39 = f32[128,2048]{0,1:T(8,128)} fusion(f32[128,4096]{1,0:T(8,128)} %fusion.27, bf16[4096,2048]{1,0:T(8,128)(2,1)} %param.8, bf16[512,8,16,128]{3,2,1,0:T(8,128)(2,1)} %bitcast.88), kind=kOutput, calls=%fused_computation.64 | convolution fusion | flops 12893290496 | bytes 36700160 | tf_op jit(solution)/shard_map/dot_general | solution.py:57
  310.9 3.9 fusion.43
  314.9 2.0 convolution_subtract_fusion
  316.9 0.5 all-reduce.14.cloned.1.call-start
  317.4 77.8 %all-reduce.12.cloned.1.call-done = f32[128,2048]{0,1:T(8,128)} async-done(((f32[128,2048]{0,1:T(8,128)}), f32[128,2048]{0,1:T(8,128)}) %all-reduce.12.cloned.1.call-update) | async-done | bytes 1048592 | tf_op jit(solution)/shard_map/psum | solution.py:56
  395.2 6.4 %fusion.2 = f32[256,256]{1,0:T(8,128)} fusion(f32[128,2048]{0,1:T(8,128)} %all-reduce.12.cloned.1.call-done, f32[128,2048]{0,1:T(8,128)} %all-reduce.8.cloned.1.call-done), kind=kOutput, calls=%fused_computation.8 | convolution fusion | flops 1611137024 | bytes 2359296 | tf_op jit(solution)/shard_map/dot_general | solution.py:22
  401.6 32.0 %all-reduce.14.cloned.1.call-done = f32[256,256]{1,0:T(8,128)} async-done(((f32[256,256]{1,0:T(8,128)}), f32[256,256]{1,0:T(8,128)}) %all-reduce.14.cloned.1.call-update) | async-done | bytes 262160 | tf_op jit(solution)/shard_map/psum | solution.py:62
  433.6 1.3 fusion.14
  435.0 0.4 fusion.44
  435.5 11.7 %cholesky.85 = f32[128,128]{1,0:T(8,128)S(1)} custom-call(f32[128,128]{1,0:T(8,128)S(1)} %fusion.26), custom_call_target="Cholesky" | custom-call | tf_op jit(solution)/shard_map/jit(cholesky)/cholesky | solution.py:68
  447.2 0.6 compare_reduce_fusion.2
  447.9 0.7 fusion.16
  448.5 9.8 %custom-call.12 = f32[1,128,128]{1,2,0:T(8,128)S(1)} custom-call(f32[1,128,128]{2,1,0:T(8,128)S(1)} %fusion.16), custom_call_target="InvertDiagBlocksLowerTriangular" | custom-call | tf_op jit(solution)/shard_map/jit(_solve_triangular)/triangular_solve | solution.py:69
  458.7 1.4 fusion.38
  460.0 0.4 fusion.45
  460.5 11.9 %cholesky.96 = f32[128,128]{1,0:T(8,128)S(1)} custom-call(f32[128,128]{1,0:T(8,128)S(1)} %fusion.24), custom_call_target="Cholesky" | custom-call | tf_op jit(solution)/shard_map/jit(cholesky)/cholesky | solution.py:68
  472.5 0.6 compare_reduce_fusion.1
  473.1 0.7 fusion.17
  473.8 9.8 %custom-call.13 = f32[1,128,128]{1,2,0:T(8,128)S(1)} custom-call(f32[1,128,128]{2,1,0:T(8,128)S(1)} %fusion.17), custom_call_target="InvertDiagBlocksLowerTriangular" | custom-call | tf_op jit(solution)/shard_map/jit(_solve_triangular)/triangular_solve | solution.py:69
  483.9 0.4 fusion.37
  484.3 0.4 fusion.46
  484.8 11.7 %cholesky.107 = f32[128,128]{1,0:T(8,128)S(1)} custom-call(f32[128,128]{1,0:T(8,128)S(1)} %fusion.22), custom_call_target="Cholesky" | custom-call | tf_op jit(solution)/shard_map/jit(cholesky)/cholesky | solution.py:68
  496.6 0.6 compare_reduce_fusion
  497.2 0.7 fusion.18
  497.9 10.0 %custom-call.14 = f32[1,128,128]{1,2,0:T(8,128)S(1)} custom-call(f32[1,128,128]{2,1,0:T(8,128)S(1)} %fusion.18), custom_call_target="InvertDiagBlocksLowerTriangular" | custom-call | tf_op jit(solution)/shard_map/jit(_solve_triangular)/triangular_solve | solution.py:69
  508.2 0.6 fusion.6
  508.8 0.5 sqrt.3
  509.3 2.0 convolution_bitcast_fusion
  511.3 2.1 fusion
  513.4 1.8 copy.15
  (40 shorter events, 1.9 us)
Async XLA Ops:
  7.2 34.2 %copy-start = (bf16[2048,128]{1,0:T(8,128)(2,1)S(1)}, bf16[2048,128]{1,0:T(8,128)(2,1)}, u32[]{:S(2)}) copy-start(bf16[2048,128]{1,0:T(8,128)(2,1)} %param.11) | copy-start | bytes 1572868
  7.2 115.3 %all-reduce.8.cloned.1.call-start = ((), (), s32[]{:S(2)}) async-start(), calls=%async_computation | async-start | bytes 2097152 | tf_op jit(solution)/shard_map/psum | solution.py:46
  8.1 19.0 %copy-start.1 = (f32[4096,128]{1,0:T(8,128)S(1)}, f32[4096,128]{1,0:T(8,128)}, u32[]{:S(2)}) copy-start(f32[4096,128]{1,0:T(8,128)} %param.9) | copy-start | bytes 6291460
  41.3 136.4 %all-reduce.16.cloned.1.call-start = ((), (), s32[]{:S(2)}) async-start(), calls=%async_computation.4 | async-start | bytes 4325376 | tf_op jit(solution)/shard_map/psum | solution.py:50
  125.4 129.9 %all-reduce.10.cloned.1.call-start = ((), (), s32[]{:S(2)}) async-start(), calls=%async_computation.1 | async-start | bytes 131072 | tf_op jit(solution)/shard_map/psum | solution.py:52
  185.8 209.4 %all-reduce.12.cloned.1.call-start = ((), (), s32[]{:S(2)}) async-start(), calls=%async_computation.2 | async-start | bytes 2097152 | tf_op jit(solution)/shard_map/psum | solution.py:56
  283.2 27.7 %copy-start.2 = (f32[4096,128]{1,0:T(8,128)S(1)}, f32[4096,128]{1,0:T(8,128)}, u32[]{:S(2)}) copy-start(f32[4096,128]{1,0:T(8,128)} %param.9) | copy-start | bytes 6291460
  310.9 3.9 copy-start.4
  310.9 3.9 copy-start.6
  316.9 84.7 %copy-start.7 = (f32[128]{0:T(128)S(1)}, f32[128]{0:T(128)}, u32[]{:S(2)}) copy-start(f32[128]{0:T(128)} %param.10) | copy-start | bytes 1540
  316.9 116.7 %all-reduce.14.cloned.1.call-start = ((), (), s32[]{:S(2)}) async-start(), calls=%async_computation.3 | async-start | bytes 524288 | tf_op jit(solution)/shard_map/psum | solution.py:62
  433.6 50.3 %copy-start.5 = (f32[256,256]{1,0:T(8,128)S(1)}, f32[256,256]{1,0:T(8,128)}, u32[]{:S(2)}) copy-start(f32[256,256]{1,0:T(8,128)} %all-reduce.14.cloned.1.call-done) | copy-start | bytes 786436
  509.3 2.0 copy-start.3
Sparse Core Ops, SparseCore 0:
  41.4 81.0 all-reduce.7
  125.6 52.0 all-reduce.15
  185.9 69.3 all-reduce.9
  317.0 78.1 all-reduce.11
  401.7 31.8 all-reduce.13
where the time goes:
time: 529 us; the launch traced here: 522 us
  waiting for transfers between devices  296 us (56%)
  matrix products  93.8 us (18%)
  other arithmetic  93.4 us (18%)
  local copies, waits for them, and re-layouts  22.7 us (4%)
  between operations  14.3 us (3%)
    psum x1, waiting for transfers between devices, local(): lax.psum(jnp.dot(basis_rows, masked, precision=highest, preferred_element...  77.8 us
    psum x1, waiting for transfers between devices, local(): sketch_gram = lax.psum(contract(sketch, sketch), 'gene')  69.3 us
    psum x1, waiting for transfers between devices, local(): projection = lax.psum(proj_part, 'gene')  65.6 us
    psum x1, waiting for transfers between devices, local(): raw_sketch, small_sketch = lax.psum((raw_part, small_part), 'cell')  51.7 us
    another operation x9, other arithmetic, local(): chol = jnp.linalg.cholesky(contract(image_block, image_block))  37.3 us
    psum x1, waiting for transfers between devices, local(): core_sum = lax.psum(outer_rows(stacked), 'cell')  32 us
    another operation x6, other arithmetic, local(): jax.scipy.linalg.solve_triangular(chol, image_block.T, lower=True)  31.6 us
    dot_general x1, matrix products, local(): jnp.dot(basis_rows, masked, precision=highest, preferred_element_type=jnp...  27.7 us
  transfers between devices with their start and end apart: 5, of which 5 were waited for; matrix products, arithmetic and copies ran while one was open for 3% of the time, Pallas kernels for 0%

commit v1 on v0

--- a/solution.py
+++ b/solution.py
@@ -49,7 +49,9 @@
     small_part = jnp.dot(projection, test_wide, precision=highest)
     raw_sketch, small_sketch = lax.psum((raw_part, small_part), "cell")
     sketch = raw_sketch - jnp.dot(loadings, small_sketch, precision=highest)
-    sketch_gram = lax.psum(contract(sketch, sketch), "gene")
+    own = contract(sketch, sketch)
+    parts = lax.all_gather(own, "gene", axis=0, tiled=False)
+    sketch_gram = parts.sum(axis=0)
     factor = jnp.linalg.cholesky(sketch_gram)
     basis_rows = jax.scipy.linalg.solve_triangular(factor, sketch.T, lower=True)
     along_loadings = jnp.dot(basis_rows, loadings, precision=highest)

time: 529 us -> 489 us (0.924)
  waiting for transfers between devices: 296 us -> 227 us
  blocking collectives: 0 us -> 31.7 us
    psum x1 -> x0, waiting for transfers between devices: 69.3 us -> none  [local(): sketch_gram = lax.psum(contract(sketch, sketch), 'gene')]
    all_gather x0 -> x1, blocking collectives: none -> 31.7 us  [local(): parts = lax.all_gather(own, 'gene', axis=0, tiled=False)]
  transfers between devices with their start and end apart: 5 -> 4, of which waited for: 5 -> 4; matrix products, arithmetic and copies ran while one was open for 3% -> 3% of each run, Pallas kernels for 0% -> 0%
where the time goes in v1:
time: 489 us; the launch traced here: 482 us
  waiting for transfers between devices  227 us (46%)
  matrix products  93.1 us (19%)
  other arithmetic  92.6 us (19%)
  blocking collectives  31.7 us (6%)
  local copies, waits for them, and re-layouts  21.8 us (4%)
  between operations  14.3 us (3%)
    psum x1, waiting for transfers between devices, local(): lax.psum(jnp.dot(basis_rows, masked, precision=highest, preferred_element...  77.8 us
    psum x1, waiting for transfers between devices, local(): projection = lax.psum(proj_part, 'gene')  65.5 us
    psum x1, waiting for transfers between devices, local(): raw_sketch, small_sketch = lax.psum((raw_part, small_part), 'cell')  51.7 us
    another operation x9, other arithmetic, local(): chol = jnp.linalg.cholesky(contract(image_block, image_block))  37.3 us
    psum x1, waiting for transfers between devices, local(): core_sum = lax.psum(outer_rows(stacked), 'cell')  32 us
    all_gather x1, blocking collectives, local(): parts = lax.all_gather(own, 'gene', axis=0, tiled=False)  31.7 us
    another operation x6, other arithmetic, local(): jax.scipy.linalg.solve_triangular(chol, image_block.T, lower=True)  31.6 us
    dot_general x1, matrix products, local(): jnp.dot(basis_rows, masked, precision=highest, preferred_element_type=jnp...  27.7 us
  transfers between devices with their start and end apart: 4, of which 4 were waited for; matrix products, arithmetic and copies ran while one was open for 3% of the time, Pallas kernels for 0%

profile of v1, /device:TPU:0, one launch (start us, length us, event | category | flops | bytes accessed | tf_op | source)
XLA Modules:
  0.0 481.8 jit_solution(9788520644005061528)
XLA Ops:
  7.2 0.7 convert_element_type.8
  8.1 19.0 %broadcast_in_dim.27 = bf16[4096,16,128]{2,1,0:T(8,128)(2,1)} broadcast(bf16[4096,16]{1,0:T(8,128)(2,1)S(1)} %bitcast.90), dimensions={0,1} | broadcast | bytes 16908288 | tf_op jit(solution)/shard_map/broadcast_in_dim | solution.py:38
  27.1 14.1 %convolution_bitcast_fusion.2 = f32[128,2048]{0,1:T(8,128)} fusion(f32[4096,128]{1,0:T(8,128)S(1)} %copy-done.1, bf16[4096,2048]{1,0:T(8,128)(2,1)} %param.8, bf16[512,8,16,128]{3,2,1,0:T(8,128)(2,1)} %bitcast.87), kind=kOutput, calls=%fused_computation.7 | convolution fusion | flops 2156396544 | bytes 36700160 | tf_op jit(solution)/shard_map/dot_general | solution.py:43
  41.3 15.6 %fusion.40 = f32[4096,128]{1,0:T(8,128)} fusion(bf16[2048,128]{1,0:T(8,128)(2,1)S(1)} %copy-done, bf16[4096,2048]{1,0:T(8,128)(2,1)} %param.8, bf16[512,8,16,128]{3,2,1,0:T(8,128)(2,1)} %bitcast.88), kind=kOutput, calls=%fused_computation.65 | convolution fusion | flops 2155872256 | bytes 36175872 | tf_op jit(solution)/shard_map/dot_general | solution.py:48
  56.9 65.5 %all-reduce.7.cloned.1.call-done = f32[128,2048]{0,1:T(8,128)} async-done(((f32[128,2048]{0,1:T(8,128)}), f32[128,2048]{0,1:T(8,128)}) %all-reduce.7.cloned.1.call-update) | async-done | bytes 1048592 | tf_op jit(solution)/shard_map/psum | solution.py:46
  122.4 2.8 fusion.41
  125.3 0.6 all-reduce.9.cloned.1.call-start
  125.8 51.7 %all-reduce.13.cloned.1.call-done = (f32[4096,128]{1,0:T(8,128)}, f32[128,128]{1,0:T(8,128)}) async-done(((f32[4096,128]{1,0:T(8,128)}, f32[128,128]{1,0:T(8,128)}), (f32[4096,128]{1,0:T(8,128)}, f32[128,128]{1,0:T(8,128)})) %all-reduce.13.cloned.1.call-update) | async-done | bytes 2162704 | tf_op jit(solution)/shard_map/psum | solution.py:50
  177.6 4.0 fusion.1
  181.6 3.5 fusion.42
  185.1 31.7 %all-gather = f32[1024,128]{1,0:T(8,128)S(1)} all-gather(f32[128,128]{1,0:T(8,128)S(1)} %fusion.42), channel_id=2, replica_groups=mesh['gene'=8,'cell'=4] {'gene'}, dimensions={0}, use_global_device_ids=true | all-gather | bytes 589824 | tf_op jit(solution)/shard_map/all_gather | solution.py:53
  217.0 11.7 %cholesky.74 = f32[128,128]{1,0:T(8,128)S(1)} custom-call(f32[128,128]{1,0:T(8,128)S(1)} %fusion.29), custom_call_target="Cholesky" | custom-call | tf_op jit(solution)/shard_map/jit(cholesky)/cholesky | solution.py:55
  228.7 0.6 compare_reduce_fusion.3
  229.3 0.7 fusion.15
  230.0 9.8 %custom-call.9 = f32[1,128,128]{1,2,0:T(8,128)S(1)} custom-call(f32[1,128,128]{2,1,0:T(8,128)S(1)} %fusion.15), custom_call_target="InvertDiagBlocksLowerTriangular" | custom-call | tf_op jit(solution)/shard_map/jit(_solve_triangular)/triangular_solve | solution.py:56
  239.8 3.3 fusion.27
  243.1 27.7 %fusion.39 = f32[128,2048]{0,1:T(8,128)} fusion(f32[128,4096]{1,0:T(8,128)} %fusion.27, bf16[4096,2048]{1,0:T(8,128)(2,1)} %param.8, bf16[512,8,16,128]{3,2,1,0:T(8,128)(2,1)} %bitcast.89), kind=kOutput, calls=%fused_computation.64 | convolution fusion | flops 12893290496 | bytes 36700160 | tf_op jit(solution)/shard_map/dot_general | solution.py:59
  270.8 3.9 fusion.43
  274.7 2.0 convolution_subtract_fusion
  276.7 0.5 all-reduce.11.cloned.1.call-start
  277.3 77.8 %all-reduce.9.cloned.1.call-done = f32[128,2048]{0,1:T(8,128)} async-done(((f32[128,2048]{0,1:T(8,128)}), f32[128,2048]{0,1:T(8,128)}) %all-reduce.9.cloned.1.call-update) | async-done | bytes 1048592 | tf_op jit(solution)/shard_map/psum | solution.py:58
  355.0 6.4 %fusion.2 = f32[256,256]{1,0:T(8,128)} fusion(f32[128,2048]{0,1:T(8,128)} %all-reduce.9.cloned.1.call-done, f32[128,2048]{0,1:T(8,128)} %all-reduce.7.cloned.1.call-done), kind=kOutput, calls=%fused_computation.8 | convolution fusion | flops 1611137024 | bytes 2359296 | tf_op jit(solution)/shard_map/dot_general | solution.py:22
  361.5 32.0 %all-reduce.11.cloned.1.call-done = f32[256,256]{1,0:T(8,128)} async-done(((f32[256,256]{1,0:T(8,128)}), f32[256,256]{1,0:T(8,128)}) %all-reduce.11.cloned.1.call-update) | async-done | bytes 262160 | tf_op jit(solution)/shard_map/psum | solution.py:64
  393.5 1.3 fusion.14
  394.8 0.4 fusion.44
  395.3 11.7 %cholesky.85 = f32[128,128]{1,0:T(8,128)S(1)} custom-call(f32[128,128]{1,0:T(8,128)S(1)} %fusion.26), custom_call_target="Cholesky" | custom-call | tf_op jit(solution)/shard_map/jit(cholesky)/cholesky | solution.py:70
  407.1 0.6 compare_reduce_fusion.2
  407.7 0.7 fusion.16
  408.4 9.8 %custom-call.12 = f32[1,128,128]{1,2,0:T(8,128)S(1)} custom-call(f32[1,128,128]{2,1,0:T(8,128)S(1)} %fusion.16), custom_call_target="InvertDiagBlocksLowerTriangular" | custom-call | tf_op jit(solution)/shard_map/jit(_solve_triangular)/triangular_solve | solution.py:71
  418.2 0.3 fusion.12
  418.5 1.4 fusion.38
  419.9 0.4 fusion.45
  420.4 11.9 %cholesky.96 = f32[128,128]{1,0:T(8,128)S(1)} custom-call(f32[128,128]{1,0:T(8,128)S(1)} %fusion.24), custom_call_target="Cholesky" | custom-call | tf_op jit(solution)/shard_map/jit(cholesky)/cholesky | solution.py:70
  432.3 0.6 compare_reduce_fusion.1
  432.9 0.7 fusion.17
  433.6 9.8 %custom-call.13 = f32[1,128,128]{1,2,0:T(8,128)S(1)} custom-call(f32[1,128,128]{2,1,0:T(8,128)S(1)} %fusion.17), custom_call_target="InvertDiagBlocksLowerTriangular" | custom-call | tf_op jit(solution)/shard_map/jit(_solve_triangular)/triangular_solve | solution.py:71
  443.4 0.3 fusion.10
  443.7 0.4 fusion.37
  444.2 0.4 fusion.46
  444.7 11.7 %cholesky.107 = f32[128,128]{1,0:T(8,128)S(1)} custom-call(f32[128,128]{1,0:T(8,128)S(1)} %fusion.22), custom_call_target="Cholesky" | custom-call | tf_op jit(solution)/shard_map/jit(cholesky)/cholesky | solution.py:70
  456.4 0.6 compare_reduce_fusion
  457.0 0.7 fusion.18
  457.7 10.0 %custom-call.14 = f32[1,128,128]{1,2,0:T(8,128)S(1)} custom-call(f32[1,128,128]{2,1,0:T(8,128)S(1)} %fusion.18), custom_call_target="InvertDiagBlocksLowerTriangular" | custom-call | tf_op jit(solution)/shard_map/jit(_solve_triangular)/triangular_solve | solution.py:71
  468.0 0.6 fusion.6
  468.6 0.5 sqrt.3
  469.1 2.0 convolution_bitcast_fusion
  471.1 2.1 fusion
  473.2 1.8 copy.22
  (39 shorter events, 1.2 us)
Async XLA Ops:
  7.2 34.1 %copy-start = (bf16[2048,128]{1,0:T(8,128)(2,1)S(1)}, bf16[2048,128]{1,0:T(8,128)(2,1)}, u32[]{:S(2)}) copy-start(bf16[2048,128]{1,0:T(8,128)(2,1)} %param.11) | copy-start | bytes 1572868
  7.2 115.2 %all-reduce.7.cloned.1.call-start = ((), (), s32[]{:S(2)}) async-start(), calls=%async_computation | async-start | bytes 2097152 | tf_op jit(solution)/shard_map/psum | solution.py:46
  8.1 19.0 %copy-start.1 = (f32[4096,128]{1,0:T(8,128)S(1)}, f32[4096,128]{1,0:T(8,128)}, u32[]{:S(2)}) copy-start(f32[4096,128]{1,0:T(8,128)} %param.9) | copy-start | bytes 6291460
  41.2 136.4 %all-reduce.13.cloned.1.call-start = ((), (), s32[]{:S(2)}) async-start(), calls=%async_computation.3 | async-start | bytes 4325376 | tf_op jit(solution)/shard_map/psum | solution.py:50
  125.3 229.8 %all-reduce.9.cloned.1.call-start = ((), (), s32[]{:S(2)}) async-start(), calls=%async_computation.1 | async-start | bytes 2097152 | tf_op jit(solution)/shard_map/psum | solution.py:58
  243.1 27.7 %copy-start.2 = (f32[4096,128]{1,0:T(8,128)S(1)}, f32[4096,128]{1,0:T(8,128)}, u32[]{:S(2)}) copy-start(f32[4096,128]{1,0:T(8,128)} %param.9) | copy-start | bytes 6291460
  270.8 3.9 copy-start.4
  270.8 3.9 copy-start.6
  276.7 84.7 %copy-start.7 = (f32[128]{0:T(128)S(1)}, f32[128]{0:T(128)}, u32[]{:S(2)}) copy-start(f32[128]{0:T(128)} %param.10) | copy-start | bytes 1540
  276.7 116.7 %all-reduce.11.cloned.1.call-start = ((), (), s32[]{:S(2)}) async-start(), calls=%async_computation.2 | async-start | bytes 524288 | tf_op jit(solution)/shard_map/psum | solution.py:64
  393.5 50.3 %copy-start.5 = (f32[256,256]{1,0:T(8,128)S(1)}, f32[256,256]{1,0:T(8,128)}, u32[]{:S(2)}) copy-start(f32[256,256]{1,0:T(8,128)} %all-reduce.11.cloned.1.call-done) | copy-start | bytes 786436
  469.1 2.0 copy-start.3
Sparse Core Ops, SparseCore 0:
  41.3 81.0 all-reduce.6
  125.5 52.0 all-reduce.12
  276.9 78.1 all-reduce.8
  361.5 31.8 all-reduce.10
